TPU v7x, 1024 devices: a whole 8x8x8 slice. The times are simulated.
1024 devices in a mesh: rows: 1024 (over z, y, x, core).
Axes of the slice: x: 8, y: 8, z: 8, core: 2. Of those that a mesh axis runs over, the one named last changes fastest.
Arguments:
- snapshots: float32 [524288, 512], P('rows'), may hold values from -100 to 100
- validation: float32 [524288, 512], P('rows'), may hold values from -100 to 100
- eigenvectors: float32 [512, 64], replicated, may hold values from -0.25 to 0.25
- eigenvalues: float32 [64], replicated, may hold values from 16 to 256
Outputs:
- gram: float32 [512, 512], replicated
- modes: float32 [64, 524288], P(None, 'rows')
- train_coef: float32 [64, 512], replicated
- valid_coef: float32 [64, 512], replicated
All inputs are finite; a program needn't handle non-finite values.
Results may differ from a plain program's by a relative error of at most 0.000071.
Values sent between devices are 32-bit elements; how exact they have to be, the bound alone decides.
A program may use at most 32 MiB of HBM per device.

v0:
```python
import jax
import jax.numpy as jnp
from jax import lax
from jax.sharding import PartitionSpec as P


def body(snapshots, validation, eigenvectors, eigenvalues):
    highest = lax.Precision.HIGHEST
    devices = lax.axis_size("rows")
    total = snapshots.shape[0] * devices * 1.0
    gram_part = (
        lax.dot_general(
            snapshots,
            snapshots,
            (((0,), (0,)), ((), ())),
            precision=highest,
            preferred_element_type=jnp.float32,
        )
        / total
    )
    scales = lax.rsqrt(eigenvalues)
    modes = (
        lax.dot_general(
            eigenvectors,
            snapshots,
            (((0,), (1,)), ((), ())),
            precision=highest,
            preferred_element_type=jnp.float32,
        )
        * scales[:, None]
    )
    gram = lax.psum(gram_part, "rows")
    valid_part = (
        jnp.dot(modes, validation, precision=highest, preferred_element_type=jnp.float32) / total
    )
    valid_coef = lax.psum(valid_part, "rows")
    train_coef = (
        lax.dot_general(
            eigenvectors,
            gram,
            (((0,), (0,)), ((), ())),
            precision=highest,
            preferred_element_type=jnp.float32,
        )
        * scales[:, None]
    )
    return (gram, modes, train_coef, valid_coef)


def solution(mesh):
    in_specs = (P("rows", None), P("rows", None), P(), P())
    out_specs = (P(), P(None, "rows"), P(), P())
    return jax.shard_map(body, mesh=mesh, in_specs=in_specs, out_specs=out_specs, check_vma=False)
```

profile of v0, /device:TPU:1, one launch (start us, length us, event | category | flops | bytes accessed | tf_op | source)
XLA Modules:
  0.0 330.9 jit_solution(9655374363504949384)
XLA Ops:
  7.2 0.0 copy-start
  7.2 0.0 all-reduce.3.cloned.1.call-start
  7.2 0.7 rsqrt.3
  8.0 0.4 copy-done
  8.4 0.0 copy-start.3
  8.4 2.8 convolution_multiply_fusion
  11.2 0.0 copy-done.3
  11.2 0.0 copy-start.2
  11.2 1.1 convolution_multiply_fusion.3
  12.4 0.1 copy-done.2
  12.5 0.0 copy-start.4
  12.5 1.4 convolution_multiply_fusion.1
  13.9 0.0 copy-done.4
  13.9 0.0 all-reduce.3.cloned.1.call-update
  13.9 305.7 %all-reduce.3.cloned.1.call-done = (f32[512,512]{1,0:T(8,128)}, f32[64,512]{1,0:T(8,128)}) async-done(((f32[512,512]{1,0:T(8,128)}, f32[64,512]{1,0:T(8,128)}), (f32[512,512]{1,0:T(8,128)}, f32[64,512]{1,0:T(8,128)})) %all-reduce.3.cloned.1.call-update) | async-done | bytes 1179664 | tf_op jit(solution)/shard_map/psum | solution.py:32
  319.7 0.0 copy-start.1
  319.7 2.8 fusion
  322.4 0.0 copy-done.1
  322.4 0.0 copy-start.5
  322.4 1.0 copy.10
  323.4 0.1 copy-done.5
  323.4 0.7 copy.11
Async XLA Ops:
  7.2 1.2 copy-start
  7.2 312.5 %all-reduce.3.cloned.1.call-start = ((), (), s32[]{:S(2)}) async-start(), calls=%async_computation | async-start | bytes 2359296 | tf_op jit(solution)/shard_map/psum | solution.py:32
  8.4 2.8 copy-start.3
  11.2 1.2 copy-start.2
  12.5 1.4 copy-start.4
  319.7 2.8 copy-start.1
  322.4 1.0 copy-start.5
Sparse Core Ops, SparseCore 0:
  14.0 305.5 all-reduce.2
where the time goes:
time: 331 us
  waiting for transfers between devices  306 us (92%)
  between operations  14 us (4%)
  matrix products  8.12 us (2%)
    psum x1, waiting for transfers between devices, body(): gram = lax.psum(gram_part, 'rows')  306 us
  transfers between devices with their start and end apart: 1, of which 1 were waited for; matrix products, arithmetic and copies ran while one was open for 0% of the time, Pallas kernels for 0%

commit v1 on v0

v1 whole, which is shorter than its diff:
```python
import functools

import jax
import jax.numpy as jnp
from jax import lax
from jax.experimental import pallas as pl
from jax.experimental.pallas import tpu as pltpu
from jax.sharding import PartitionSpec as P

MESH = pl.DeviceIdType.MESH
F32 = jnp.float32
BF16 = jnp.bfloat16
UNIT = 256
BLOCKS = [(0, 0), (0, 1), (1, 1), (0, 2), (0, 3), (1, 2), (1, 3), (2, 2), (2, 3), (3, 3)]


def split(x):
    hi = x.astype(BF16)
    return hi, (x - hi.astype(F32)).astype(BF16)


def dot(a, b):
    return jnp.dot(a, b, preferred_element_type=F32)


def dot_nt(a, b):
    return lax.dot_general(a, b, (((1,), (1,)), ((), ())), preferred_element_type=F32)


def three(f, a, b):
    (ah, al), (bh, bl) = a, b
    return f(ah, bh) + (f(ah, bl) + f(al, bh))


def scaled_vectors(vec_ref, val_ref):
    return jnp.transpose(vec_ref[...] * lax.rsqrt(val_ref[...]))


def reduce_kernel(
    side, inv_total, snap_hbm, valid_hbm, vec_ref, val_ref, full_ref, modes_ref,
    snap, valid, xh, xl, xht, xlt, pay, pair, acc, ring1, mine, ring2, ring3,
    in_sem, pair_send, pair_recv, send_sem, recv_sem, last_send, last_recv,
):
    me = lax.axis_index("rows")
    core = lax.rem(me, 2)
    strides = (2, 2 * side, 2 * side * side)
    spots = [lax.rem(me // s, side) for s in strides]
    partner = me + 1 - 2 * core
    piece = UNIT // side

    def peer(axis, d):
        return me + (lax.rem(spots[axis] + d, side) - spots[axis]) * strides[axis]

    def each(f):
        def step(d, carry):
            f(d)
            return carry

        lax.fori_loop(1, side, step, 0)

    barrier = pltpu.get_barrier_semaphore()
    for axis in range(3):
        each(
            lambda d, axis=axis: pl.semaphore_signal(
                barrier, inc=1, device_id=(peer(axis, d),), device_id_type=MESH
            )
        )
    pl.semaphore_signal(barrier, inc=1, device_id=(partner,), device_id_type=MESH)

    load_snap = pltpu.make_async_copy(snap_hbm, snap, in_sem.at[0])
    load_valid = pltpu.make_async_copy(valid_hbm, valid, in_sem.at[1])
    load_snap.start()
    load_valid.start()
    load_snap.wait()

    h, l = split(snap[...])
    xh[...] = h
    xl[...] = l
    xht[...] = jnp.transpose(h)
    xlt[...] = jnp.transpose(l)
    for big, (p, q) in enumerate([(0, 0), (0, 1), (1, 1)]):
        rows, cols = pl.ds(p * 256, 256), pl.ds(q * 256, 256)
        g = three(dot, (xht[rows, :], xlt[rows, :]), (xh[:, cols], xl[:, cols])) * inv_total
        for k, (i, j) in enumerate(BLOCKS):
            if (i // 2, j // 2) == (p, q):
                r, c = 128 * (i % 2), 128 * (j % 2)
                pay[k // 2, pl.ds(128 * (k % 2), 128), :] = g[r : r + 128, c : c + 128]
    vectors = split(scaled_vectors(vec_ref, val_ref))
    modes = three(dot_nt, vectors, (xh[...], xl[...]))
    modes_ref[...] = modes
    load_valid.wait()
    part = three(dot, split(modes), split(valid[...])) * inv_total
    for j in range(4):
        pay[5, pl.ds(64 * j, 64), :] = part[:, 128 * j : 128 * j + 128]

    pl.semaphore_wait(barrier, 3 * (side - 1) + 1)

    pairs = []
    for t in range(3):
        c = pltpu.make_async_remote_copy(
            src_ref=pay.at[2 * t + 1 - core], dst_ref=pair.at[t],
            send_sem=pair_send.at[t], recv_sem=pair_recv.at[t],
            device_id=(partner,), device_id_type=MESH,
        )
        c.start()
        pairs.append(c)

    def rows_of(k):
        return pl.ds(pl.multiple_of(k * piece, piece), piece)

    def copy(stage, t, d):
        axis = (t + (0, 1, 2, 0)[stage]) % 3
        spot = spots[axis]
        if stage == 0:
            src = acc.at[t, rows_of(lax.rem(spot + d, side)), :]
            dst = ring1.at[t, d - 1]
        elif stage == 1:
            src, dst = mine.at[t], ring2.at[t, spot]
        elif stage == 2:
            src, dst = mine.at[3 + t], ring3.at[t, spot]
        else:
            src = mine.at[6 + t]
            dst = full_ref.at[2 * t + core, rows_of(spot), :]
        k = (stage * 3 + t) * side + d
        return pltpu.make_async_remote_copy(
            src_ref=src, dst_ref=dst, send_sem=send_sem.at[k], recv_sem=recv_sem.at[k],
            device_id=(peer(axis, d),), device_id_type=MESH,
        )

    for t in range(3):
        pairs[t].wait_recv()
        acc[t] = pay[2 * t + core] + pair[t]
        each(lambda d, t=t: copy(0, t, d).start())
    for t in range(3):
        each(lambda d, t=t: copy(0, t, d).wait_recv())
        total = acc[t, rows_of(spots[t]), :]
        for d in range(side - 1):
            total += ring1[t, d]
        mine[t] = total
        ring2[t, spots[(t + 1) % 3]] = total
        each(lambda d, t=t: copy(1, t, d).start())
    for t in range(3):
        each(lambda d, t=t: copy(1, t, d).wait_recv())
        total = ring2[t, 0]
        for d in range(1, side):
            total += ring2[t, d]
        mine[3 + t] = total
        ring3[t, spots[(t + 2) % 3]] = total
        each(lambda d, t=t: copy(2, t, d).start())
    for t in range(3):
        each(lambda d, t=t: copy(2, t, d).wait_recv())
        total = ring3[t, 0]
        for d in range(1, side):
            total += ring3[t, d]
        mine[6 + t] = total
        full_ref[2 * t + core, rows_of(spots[t]), :] = total
        each(lambda d, t=t: copy(3, t, d).start())

    def last(t, d):
        spot = lax.rem(spots[t] + side - d, side)
        ref = full_ref.at[2 * t + core, rows_of(spot), :]
        src = mine.at[6 + t] if isinstance(d, int) and d == 0 else ref
        k = t * side + d
        return pltpu.make_async_remote_copy(
            src_ref=src, dst_ref=ref, send_sem=last_send.at[k], recv_sem=last_recv.at[k],
            device_id=(partner,), device_id_type=MESH,
        )

    for t in range(3):
        last(t, 0).start()
    for t in range(3):

        def forward(d, t=t):
            copy(3, t, d).wait_recv()
            last(t, d).start()

        each(forward)
    for stage in range(4):
        for t in range(3):
            each(lambda d, stage=stage, t=t: copy(stage, t, d).wait_send())
    for t in range(3):
        pairs[t].wait_send()

        def end(d, carry, t=t):
            spot = lax.rem(spots[t] + side - d, side)
            arrived = full_ref.at[2 * t + 1 - core, rows_of(spot), :]
            k = t * side + d
            c = pltpu.make_async_remote_copy(
                src_ref=arrived, dst_ref=arrived, send_sem=last_send.at[k],
                recv_sem=last_recv.at[k], device_id=(partner,), device_id_type=MESH,
            )
            c.wait_send()
            c.wait_recv()
            return carry

        lax.fori_loop(0, side, end, 0)


def finish_kernel(full_ref, vec_ref, val_ref, modes_in, gram_ref, modes_ref, train_ref, valid_ref):
    for k, (i, j) in enumerate(BLOCKS):
        b = full_ref[k // 2, pl.ds(128 * (k % 2), 128), :]
        gram_ref[pl.ds(128 * i, 128), pl.ds(128 * j, 128)] = b
        if i != j:
            gram_ref[pl.ds(128 * j, 128), pl.ds(128 * i, 128)] = jnp.transpose(b)
    for j in range(4):
        valid_ref[:, pl.ds(128 * j, 128)] = full_ref[5, pl.ds(64 * j, 64), :]
    modes_ref[...] = modes_in[...]
    train_ref[...] = three(dot, split(scaled_vectors(vec_ref, val_ref)), split(gram_ref[...]))


def body(snapshots, validation, eigenvectors, eigenvalues, *, side):
    rows, count = snapshots.shape
    modes = eigenvectors.shape[1]
    devices = 2 * side**3
    piece = UNIT // side
    values = eigenvalues.reshape(1, modes)
    vmem = pl.BlockSpec(memory_space=pltpu.VMEM)
    hbm = pl.BlockSpec(memory_space=pl.ANY)
    dma = pltpu.SemaphoreType.DMA
    full, modes_part = pl.pallas_call(
        functools.partial(reduce_kernel, side, 1.0 / (rows * devices)),
        out_shape=(
            jax.ShapeDtypeStruct((6, UNIT, 128), F32),
            jax.ShapeDtypeStruct((modes, rows), F32),
        ),
        in_specs=[hbm, hbm, vmem, vmem],
        out_specs=(vmem, vmem),
        scratch_shapes=[
            pltpu.VMEM((rows, count), F32),
            pltpu.VMEM((rows, count), F32),
            pltpu.VMEM((rows, count), BF16),
            pltpu.VMEM((rows, count), BF16),
            pltpu.VMEM((count, rows), BF16),
            pltpu.VMEM((count, rows), BF16),
            pltpu.VMEM((6, UNIT, 128), F32),
            pltpu.VMEM((3, UNIT, 128), F32),
            pltpu.VMEM((3, UNIT, 128), F32),
            pltpu.VMEM((3, side - 1, piece, 128), F32),
            pltpu.VMEM((9, piece, 128), F32),
            pltpu.VMEM((3, side, piece, 128), F32),
            pltpu.VMEM((3, side, piece, 128), F32),
            dma((2,)),
            dma((3,)),
            dma((3,)),
            dma((12 * side,)),
            dma((12 * side,)),
            dma((3 * side,)),
            dma((3 * side,)),
        ],
        compiler_params=pltpu.CompilerParams(collective_id=0, has_side_effects=True),
        name="reduce",
    )(snapshots, validation, eigenvectors, values)
    return pl.pallas_call(
        finish_kernel,
        out_shape=(
            jax.ShapeDtypeStruct((count, count), F32),
            jax.ShapeDtypeStruct((modes, rows), F32),
            jax.ShapeDtypeStruct((modes, count), F32),
            jax.ShapeDtypeStruct((modes, count), F32),
        ),
        in_specs=[vmem] * 4,
        out_specs=(vmem,) * 4,
        name="finish",
    )(full, eigenvectors, values, modes_part)


def solution(mesh):
    side = round((mesh.shape["rows"] // 2) ** (1 / 3))
    in_specs = (P("rows", None), P("rows", None), P(), P())
    out_specs = (P(), P(None, "rows"), P(), P())
    return jax.shard_map(
        functools.partial(body, side=side),
        mesh=mesh,
        in_specs=in_specs,
        out_specs=out_specs,
        check_vma=False,
    )
```

time: 331 us -> 60.6 us (0.18)
  waiting for transfers between devices: 306 us -> 0 us
  Pallas kernels: 0 us -> 58 us
  between operations: 14 us -> 0.64 us
  matrix products: 8.12 us -> 0 us
    psum x1 -> x0, waiting for transfers between devices: 306 us -> none  [body(): gram = lax.psum(gram_part, 'rows')]
    pallas_call x0 -> x2, Pallas kernels: none -> 58 us  [the longest x1 55.4 us: body(): pl.pallas_call(functools.partial(reduce_kernel, side, 1.0 / (rows * devic...]
    dot_general x4 -> x0, matrix products: 8.12 us -> none  [the longest x1 2.83 us: body(): lax.dot_general(snapshots, snapshots, (((0,), (0,)), ((), ())), precision...]
  transfers between devices with their start and end apart: 1 -> 0, of which waited for: 1 -> 0; matrix products, arithmetic and copies ran while one was open for 0% -> 0% of each run, Pallas kernels for 0% -> 0%
where the time goes in v1:
time: 60.6 us; the launch traced here: 60.3 us
  Pallas kernels  58 us (96%)
  local copies, waits for them, and re-layouts  1.74 us (3%)
  between operations  0.64 us (1%)
    pallas_call x1, Pallas kernels, body(): pl.pallas_call(functools.partial(reduce_kernel, side, 1.0 / (rows * devic...  55.4 us
    pallas_call x1, Pallas kernels, body(): pl.pallas_call(finish_kernel, out_shape=(jax.ShapeDtypeStruct((count, cou...  2.55 us
    unnamed x1, local copies, waits for them, and re-layouts  1.74 us

profile of v1, /device:TPU:1, one launch (start us, length us, event | category | flops | bytes accessed | tf_op | source)
XLA Modules:
  0.0 60.3 jit_solution(1605508341815365851)
XLA Ops:
  0.6 1.7 %copy.8.vec_ref = f32[512,64]{1,0:T(8,128)} copy(f32[512,64]{0,1:T(8,128)} %param.6) | data formatting | bytes 262144 | tf_op args[2]
  2.4 55.4 %reduce.1 = (f32[6,256,128]{2,1,0:T(8,128)}, f32[64,512]{1,0:T(8,128)}) custom-call(f32[512,512]{1,0:T(8,128)} %snap_hbm.1, f32[512,512]{1,0:T(8,128)} %valid_hbm.1, f32[512,64]{1,0:T(8,128)} %copy.8.vec_ref, f32[1,64]{1,0:T(1,128)} %bitcast.1), custom_call_target="tpu_custom_call" | custom-call | tf_op jit(solution)/shard_map/reduce/pallas_call | solution.py:220
  57.8 2.6 %finish.1 = (f32[512,512]{1,0:T(8,128)}, f32[64,512]{1,0:T(8,128)}, f32[64,512]{1,0:T(8,128)}, f32[64,512]{1,0:T(8,128)}) custom-call(f32[6,256,128]{2,1,0:T(8,128)} %get-tuple-element.6.full_ref, f32[512,64]{1,0:T(8,128)} %copy.8.vec_ref, f32[1,64]{1,0:T(1,128)} %bitcast.2, f32[64,512]{1,0:T(8,128)} %get-tuple-element.7.modes_in), custom_call_target="tpu_custom_call" | custom-call | tf_op jit(solution)/shard_map/finish/pallas_call | solution.py:253
